TPU v7x, 256 devices: a whole 4x4x8 slice. The times are simulated.
256 devices in a mesh: row: 8 (over z), col: 32 (over y, x, core).
Axes of the slice: x: 4, y: 4, z: 8, core: 2. Of those that a mesh axis runs over, the one named last changes fastest.
Arguments:
- signs: int32 [1, 4096, 4096], P(None, 'row', 'col'), may hold values from 0 to 1
- upper_a: bfloat16 [4096, 4096], P('row'), may hold values from -1 to 1, as said below
- upper_b: bfloat16 [4096, 4096], P(None, 'col'), may hold values from -1 to 1, as said below
- diag_inverse: bfloat16 [4096, 512], P('row'), may hold values from -5 to 5
Outputs:
- solved: bfloat16 [1, 4096, 4096], P(None, 'row', 'col')
- col_norms: float32 [1, 4096], P(None, 'col')
- row_peaks: float32 [1, 4096], P(None, 'row')
Inputs may be any that keep to these rules, and one draw needn't show every extreme that they name: `upper_a`: zero in every block of 512 x 512 on or below the block diagonal. `upper_b`: zero below its diagonal blocks of 128 x 128.
All inputs are finite; a program needn't handle non-finite values.
Results may differ from a plain program's by a relative error of at most 0.024.
Values may be sent and summed in bfloat16 or wider, within the bound.
A program may use at most 64 MiB of HBM per device.

v0:
```python
import jax
import jax.numpy as jnp
from jax import lax
from jax.sharding import PartitionSpec as P

SWEEPS = 3


def shifted(value, axis, steps):
    count = lax.axis_size(axis)
    leading, last = (max(0, -steps), min(count, count - steps))
    return lax.ppermute(value, axis, [(source, source + steps) for source in range(leading, last)])


def copy_for_each(value, axis):
    copies = jnp.broadcast_to(value, (lax.axis_size(axis), *value.shape))
    return lax.all_to_all(copies, axis, split_axis=0, concat_axis=0, tiled=True)


def over_copies(value, axis):
    everything = copy_for_each(value, axis)
    return jnp.max(everything, axis=0)


def shards(signs, upper_a, upper_b, diag_inverse):
    row_count = lax.axis_size("row")
    col_count = lax.axis_size("col")
    my_row = lax.axis_index("row")
    my_col = lax.axis_index("col")
    blk_rows = upper_a.shape[0]
    blk_cols = upper_b.shape[1]
    diag_block = lax.dynamic_slice_in_dim(upper_b, my_col * blk_cols, blk_cols, 0)
    targets = (2 * signs - 1).astype(jnp.float32)

    def solve_block(residual):
        estimate = jnp.einsum(
            "ij,pjk->pik",
            diag_inverse,
            residual.astype(jnp.bfloat16),
            preferred_element_type=jnp.float32,
        ).astype(jnp.bfloat16)
        for number in range(SWEEPS):
            remainder = residual - jnp.einsum(
                "pij,jk->pik", estimate, diag_block, preferred_element_type=jnp.float32
            )
            estimate = jnp.einsum(
                "ij,pjk->pik",
                diag_inverse,
                remainder.astype(jnp.bfloat16),
                preferred_element_type=jnp.float32,
            ).astype(jnp.bfloat16)
        return estimate

    def lower_update(residual, tile, source_row):
        coupling = lax.dynamic_slice_in_dim(upper_a, source_row * blk_rows, blk_rows, 1)
        return residual - jnp.einsum(
            "ij,pjk->pik", coupling, tile, preferred_element_type=jnp.float32
        )

    def left_update(residual, tile, source_col):
        coupling = lax.dynamic_slice_in_dim(upper_b, source_col * blk_cols, blk_cols, 0)
        return residual - jnp.einsum(
            "pij,jk->pik", tile, coupling, preferred_element_type=jnp.float32
        )

    def keep_first(operands):
        return operands[0]

    blocks = jnp.zeros(targets.shape, jnp.bfloat16)
    own_turn = 2 * (row_count - 1 - my_row) + 2 * my_col

    def advance(turn_index, state_tuple):
        residual, blocks, send_up, send_right = state_tuple
        active = turn_index == own_turn
        blocks = lax.cond(
            active,
            lambda operands: solve_block(operands[0]),
            lambda operands: operands[1],
            (residual, blocks),
        )
        send_up = jnp.where(active, blocks, send_up)
        send_right = jnp.where(active, blocks, send_right)
        from_below = shifted(send_up, "row", -1)
        from_left = shifted(send_right, "col", 1)
        source_row = 2 * my_col + 2 * row_count - 3 - my_row - turn_index
        row_valid = (source_row > my_row) & (source_row < row_count)
        clipped_row = jnp.clip(source_row, 0, row_count - 1)
        source_col = turn_index - 2 * (row_count - 1 - my_row) - my_col + 1
        col_valid = (source_col >= 0) & (source_col < my_col)
        clipped_col = jnp.clip(source_col, 0, col_count - 1)
        residual = lax.cond(
            row_valid,
            lambda operands: lower_update(operands[0], operands[1], clipped_row),
            keep_first,
            (residual, from_below),
        )
        residual = lax.cond(
            col_valid,
            lambda operands: left_update(operands[0], operands[1], clipped_col),
            keep_first,
            (residual, from_left),
        )
        return (residual, blocks, from_below, from_left)

    state_tuple = lax.fori_loop(
        0, 2 * row_count + 2 * col_count - 3, advance, (targets, blocks, blocks, blocks)
    )
    solved = state_tuple[1]
    magnitude = jnp.abs(solved.astype(jnp.float32))
    col_total = lax.psum(jnp.sum(magnitude, axis=1), "row")
    row_top = over_copies(jnp.max(magnitude, axis=2), "col")
    return (solved, col_total, row_top)


def solution(mesh):
    in_specs = (P(None, "row", "col"), P("row", None), P(None, "col"), P("row", None))
    out_specs = (P(None, "row", "col"), P(None, "col"), P(None, "row"))
    return jax.shard_map(shards, mesh=mesh, in_specs=in_specs, out_specs=out_specs, check_vma=False)
```

profile of v0, /device:TPU:1, one launch (start us, length us, event | category | flops | bytes accessed | tf_op | source)
XLA Modules:
  0.0 1039.0 jit_solution(13029806864201934861)
XLA Ops:
  3.3 912.3 %while.27 = (s32[]{:T(128)}, f32[1,512,128]{1,2,0:T(8,128)}, bf16[1,512,128]{1,2,0:T(8,128)(2,1)S(1)}, bf16[1,512,128]{2,1,0:T(8,128)(2,1)S(1)}, bf16[1,512,128]...) while((s32[]{:T(128)}, f32[1,512,128]{1,2,0:T(8,128)}, ...), condition=%wide.region_7.8_spmd, body=%wide.region_0.7_spmd.sunk | while | flops 403636224 | bytes 9306748 | solution.py:105
  89.0 9.2 collective-permute-done
  105.1 9.1 collective-permute-done
  121.2 9.2 collective-permute-done
  137.2 10.4 collective-permute-done
  154.5 9.9 collective-permute-done
  171.1 10.1 collective-permute-done
  187.9 9.3 collective-permute-done
  209.2 7.1 conditional.6
  226.1 12.1 %collective-permute-start.1 = (bf16[1,512,128]{2,1,0:T(8,128)(2,1)S(1)}, bf16[1,512,128]{2,1,0:T(8,128)(2,1)S(1)}, u32[]{:S(2)}, u32[]{:S(2)}) collective-permute-start(bf16[1,512,128]{2,1,0:T(8,128)(2,1)S(1)} %get-tuple-element.596), channel_id=1, source_target_pairs={{0,1},{1,2},{2,3},{3,4},{4,5},{5,6},{6,7},{7,8},{8,9},{9,10},{10,1... | collective-permute-start | bytes 393224 | tf_op jit(solution)/shard_map/while/body/eval_jaxpr/ppermute | solution.py:12
  242.4 11.9 %collective-permute-start.1 = (bf16[1,512,128]{2,1,0:T(8,128)(2,1)S(1)}, bf16[1,512,128]{2,1,0:T(8,128)(2,1)S(1)}, u32[]{:S(2)}, u32[]{:S(2)}) collective-permute-start(bf16[1,512,128]{2,1,0:T(8,128)(2,1)S(1)} %get-tuple-element.596), channel_id=1, source_target_pairs={{0,1},{1,2},{2,3},{3,4},{4,5},{5,6},{6,7},{7,8},{8,9},{9,10},{10,1... | collective-permute-start | bytes 393224 | tf_op jit(solution)/shard_map/while/body/eval_jaxpr/ppermute | solution.py:12
  295.7 7.4 collective-permute-start.1
  307.3 11.9 %collective-permute-start.1 = (bf16[1,512,128]{2,1,0:T(8,128)(2,1)S(1)}, bf16[1,512,128]{2,1,0:T(8,128)(2,1)S(1)}, u32[]{:S(2)}, u32[]{:S(2)}) collective-permute-start(bf16[1,512,128]{2,1,0:T(8,128)(2,1)S(1)} %get-tuple-element.596), channel_id=1, source_target_pairs={{0,1},{1,2},{2,3},{3,4},{4,5},{5,6},{6,7},{7,8},{8,9},{9,10},{10,1... | collective-permute-start | bytes 393224 | tf_op jit(solution)/shard_map/while/body/eval_jaxpr/ppermute | solution.py:12
  372.4 11.7 %collective-permute-start.1 = (bf16[1,512,128]{2,1,0:T(8,128)(2,1)S(1)}, bf16[1,512,128]{2,1,0:T(8,128)(2,1)S(1)}, u32[]{:S(2)}, u32[]{:S(2)}) collective-permute-start(bf16[1,512,128]{2,1,0:T(8,128)(2,1)S(1)} %get-tuple-element.596), channel_id=1, source_target_pairs={{0,1},{1,2},{2,3},{3,4},{4,5},{5,6},{6,7},{7,8},{8,9},{9,10},{10,1... | collective-permute-start | bytes 393224 | tf_op jit(solution)/shard_map/while/body/eval_jaxpr/ppermute | solution.py:12
  388.3 7.3 collective-permute-start.1
  428.6 14.2 %collective-permute-start.1 = (bf16[1,512,128]{2,1,0:T(8,128)(2,1)S(1)}, bf16[1,512,128]{2,1,0:T(8,128)(2,1)S(1)}, u32[]{:S(2)}, u32[]{:S(2)}) collective-permute-start(bf16[1,512,128]{2,1,0:T(8,128)(2,1)S(1)} %get-tuple-element.596), channel_id=1, source_target_pairs={{0,1},{1,2},{2,3},{3,4},{4,5},{5,6},{6,7},{7,8},{8,9},{9,10},{10,1... | collective-permute-start | bytes 393224 | tf_op jit(solution)/shard_map/while/body/eval_jaxpr/ppermute | solution.py:12
  447.0 12.2 %collective-permute-start.1 = (bf16[1,512,128]{2,1,0:T(8,128)(2,1)S(1)}, bf16[1,512,128]{2,1,0:T(8,128)(2,1)S(1)}, u32[]{:S(2)}, u32[]{:S(2)}) collective-permute-start(bf16[1,512,128]{2,1,0:T(8,128)(2,1)S(1)} %get-tuple-element.596), channel_id=1, source_target_pairs={{0,1},{1,2},{2,3},{3,4},{4,5},{5,6},{6,7},{7,8},{8,9},{9,10},{10,1... | collective-permute-start | bytes 393224 | tf_op jit(solution)/shard_map/while/body/eval_jaxpr/ppermute | solution.py:12
  463.4 8.5 collective-permute-start.1
  476.1 7.1 collective-permute-start.1
  487.4 7.1 collective-permute-start.1
  498.7 7.1 collective-permute-start.1
  521.3 7.1 collective-permute-start.1
  532.7 7.1 collective-permute-start.1
  544.0 7.1 collective-permute-start.1
  555.3 7.1 collective-permute-start.1
  566.6 7.1 collective-permute-start.1
  577.9 7.1 collective-permute-start.1
  589.2 7.1 collective-permute-start.1
  600.5 7.1 collective-permute-start.1
  611.8 7.1 collective-permute-start.1
  623.1 7.1 collective-permute-start.1
  634.4 7.1 collective-permute-start.1
  645.7 7.1 collective-permute-start.1
  657.0 7.1 collective-permute-start.1
  668.3 7.1 collective-permute-start.1
  679.6 7.1 collective-permute-start.1
  690.9 7.1 collective-permute-start.1
  702.2 7.1 collective-permute-start.1
  713.5 7.1 collective-permute-start.1
  736.1 7.1 collective-permute-start.1
  747.4 7.1 collective-permute-start.1
  758.7 7.1 collective-permute-start.1
  770.1 7.1 collective-permute-start.1
  781.4 7.1 collective-permute-start.1
  792.7 7.1 collective-permute-start.1
  804.0 7.1 collective-permute-start.1
  916.3 109.3 %all-to-all-start = ((f32[32,1,512]{2,1,0:T(1,128)}), f32[32,1,512]{2,1,0:T(1,128)S(1)}, u32[]{:S(2)}, u32[]{:S(2)}) async-start(f32[32,1,512]{2,1,0:T(1,128)} %broadcast_in_dim.7), calls=%async_computation | async-start | bytes 131072 | tf_op jit(solution)/shard_map/all_to_all | solution.py:17
  1026.4 12.0 %psum.7 = f32[1,128]{1,0:T(1,128)} all-reduce(f32[1,128]{1,0:T(1,128)S(1)} %bitcast.101), channel_id=1, replica_groups=mesh['row'=8,'col'=32] {'row'}, use_global_device_ids=true, to_apply=%region_9.10 | all-reduce | flops 128 | bytes 1024 | tf_op jit(solution)/shard_map/psum | solution.py:110
  (826 shorter events, 705.0 us)
Async XLA Ops:
  69.7 12.4 %collective-permute-start = (bf16[1,512,128]{2,1,0:T(8,128)(2,1)S(1)}, bf16[1,512,128]{2,1,0:T(8,128)(2,1)S(1)}, u32[]{:S(2)}, u32[]{:S(2)}) collective-permute-start(bf16[1,512,128]{2,1,0:T(8,128)(2,1)S(1)} %get-tuple-element.595), channel_id=1, source_target_pairs={{32,0},{64,32},{96,64},{128,96},{160,128},{192,160},{224,192},{33,... | collective-permute-start | bytes 393224 | tf_op jit(solution)/shard_map/while/body/eval_jaxpr/ppermute | solution.py:12
  71.0 13.8 %collective-permute-start.1 = (bf16[1,512,128]{2,1,0:T(8,128)(2,1)S(1)}, bf16[1,512,128]{2,1,0:T(8,128)(2,1)S(1)}, u32[]{:S(2)}, u32[]{:S(2)}) collective-permute-start(bf16[1,512,128]{2,1,0:T(8,128)(2,1)S(1)} %get-tuple-element.596), channel_id=1, source_target_pairs={{0,1},{1,2},{2,3},{3,4},{4,5},{5,6},{6,7},{7,8},{8,9},{9,10},{10,1... | collective-permute-start | bytes 393224 | tf_op jit(solution)/shard_map/while/body/eval_jaxpr/ppermute | solution.py:12
  85.7 12.4 %collective-permute-start = (bf16[1,512,128]{2,1,0:T(8,128)(2,1)S(1)}, bf16[1,512,128]{2,1,0:T(8,128)(2,1)S(1)}, u32[]{:S(2)}, u32[]{:S(2)}) collective-permute-start(bf16[1,512,128]{2,1,0:T(8,128)(2,1)S(1)} %get-tuple-element.595), channel_id=1, source_target_pairs={{32,0},{64,32},{96,64},{128,96},{160,128},{192,160},{224,192},{33,... | collective-permute-start | bytes 393224 | tf_op jit(solution)/shard_map/while/body/eval_jaxpr/ppermute | solution.py:12
  87.0 13.8 %collective-permute-start.1 = (bf16[1,512,128]{2,1,0:T(8,128)(2,1)S(1)}, bf16[1,512,128]{2,1,0:T(8,128)(2,1)S(1)}, u32[]{:S(2)}, u32[]{:S(2)}) collective-permute-start(bf16[1,512,128]{2,1,0:T(8,128)(2,1)S(1)} %get-tuple-element.596), channel_id=1, source_target_pairs={{0,1},{1,2},{2,3},{3,4},{4,5},{5,6},{6,7},{7,8},{8,9},{9,10},{10,1... | collective-permute-start | bytes 393224 | tf_op jit(solution)/shard_map/while/body/eval_jaxpr/ppermute | solution.py:12
  101.8 12.4 %collective-permute-start = (bf16[1,512,128]{2,1,0:T(8,128)(2,1)S(1)}, bf16[1,512,128]{2,1,0:T(8,128)(2,1)S(1)}, u32[]{:S(2)}, u32[]{:S(2)}) collective-permute-start(bf16[1,512,128]{2,1,0:T(8,128)(2,1)S(1)} %get-tuple-element.595), channel_id=1, source_target_pairs={{32,0},{64,32},{96,64},{128,96},{160,128},{192,160},{224,192},{33,... | collective-permute-start | bytes 393224 | tf_op jit(solution)/shard_map/while/body/eval_jaxpr/ppermute | solution.py:12
  103.1 13.8 %collective-permute-start.1 = (bf16[1,512,128]{2,1,0:T(8,128)(2,1)S(1)}, bf16[1,512,128]{2,1,0:T(8,128)(2,1)S(1)}, u32[]{:S(2)}, u32[]{:S(2)}) collective-permute-start(bf16[1,512,128]{2,1,0:T(8,128)(2,1)S(1)} %get-tuple-element.596), channel_id=1, source_target_pairs={{0,1},{1,2},{2,3},{3,4},{4,5},{5,6},{6,7},{7,8},{8,9},{9,10},{10,1... | collective-permute-start | bytes 393224 | tf_op jit(solution)/shard_map/while/body/eval_jaxpr/ppermute | solution.py:12
  117.9 12.4 %collective-permute-start = (bf16[1,512,128]{2,1,0:T(8,128)(2,1)S(1)}, bf16[1,512,128]{2,1,0:T(8,128)(2,1)S(1)}, u32[]{:S(2)}, u32[]{:S(2)}) collective-permute-start(bf16[1,512,128]{2,1,0:T(8,128)(2,1)S(1)} %get-tuple-element.595), channel_id=1, source_target_pairs={{32,0},{64,32},{96,64},{128,96},{160,128},{192,160},{224,192},{33,... | collective-permute-start | bytes 393224 | tf_op jit(solution)/shard_map/while/body/eval_jaxpr/ppermute | solution.py:12
  119.2 13.8 %collective-permute-start.1 = (bf16[1,512,128]{2,1,0:T(8,128)(2,1)S(1)}, bf16[1,512,128]{2,1,0:T(8,128)(2,1)S(1)}, u32[]{:S(2)}, u32[]{:S(2)}) collective-permute-start(bf16[1,512,128]{2,1,0:T(8,128)(2,1)S(1)} %get-tuple-element.596), channel_id=1, source_target_pairs={{0,1},{1,2},{2,3},{3,4},{4,5},{5,6},{6,7},{7,8},{8,9},{9,10},{10,1... | collective-permute-start | bytes 393224 | tf_op jit(solution)/shard_map/while/body/eval_jaxpr/ppermute | solution.py:12
  134.0 13.6 %collective-permute-start = (bf16[1,512,128]{2,1,0:T(8,128)(2,1)S(1)}, bf16[1,512,128]{2,1,0:T(8,128)(2,1)S(1)}, u32[]{:S(2)}, u32[]{:S(2)}) collective-permute-start(bf16[1,512,128]{2,1,0:T(8,128)(2,1)S(1)} %get-tuple-element.595), channel_id=1, source_target_pairs={{32,0},{64,32},{96,64},{128,96},{160,128},{192,160},{224,192},{33,... | collective-permute-start | bytes 393224 | tf_op jit(solution)/shard_map/while/body/eval_jaxpr/ppermute | solution.py:12
  135.3 15.0 %collective-permute-start.1 = (bf16[1,512,128]{2,1,0:T(8,128)(2,1)S(1)}, bf16[1,512,128]{2,1,0:T(8,128)(2,1)S(1)}, u32[]{:S(2)}, u32[]{:S(2)}) collective-permute-start(bf16[1,512,128]{2,1,0:T(8,128)(2,1)S(1)} %get-tuple-element.596), channel_id=1, source_target_pairs={{0,1},{1,2},{2,3},{3,4},{4,5},{5,6},{6,7},{7,8},{8,9},{9,10},{10,1... | collective-permute-start | bytes 393224 | tf_op jit(solution)/shard_map/while/body/eval_jaxpr/ppermute | solution.py:12
  151.3 13.2 %collective-permute-start = (bf16[1,512,128]{2,1,0:T(8,128)(2,1)S(1)}, bf16[1,512,128]{2,1,0:T(8,128)(2,1)S(1)}, u32[]{:S(2)}, u32[]{:S(2)}) collective-permute-start(bf16[1,512,128]{2,1,0:T(8,128)(2,1)S(1)} %get-tuple-element.595), channel_id=1, source_target_pairs={{32,0},{64,32},{96,64},{128,96},{160,128},{192,160},{224,192},{33,... | collective-permute-start | bytes 393224 | tf_op jit(solution)/shard_map/while/body/eval_jaxpr/ppermute | solution.py:12
  152.6 14.3 %collective-permute-start.1 = (bf16[1,512,128]{2,1,0:T(8,128)(2,1)S(1)}, bf16[1,512,128]{2,1,0:T(8,128)(2,1)S(1)}, u32[]{:S(2)}, u32[]{:S(2)}) collective-permute-start(bf16[1,512,128]{2,1,0:T(8,128)(2,1)S(1)} %get-tuple-element.596), channel_id=1, source_target_pairs={{0,1},{1,2},{2,3},{3,4},{4,5},{5,6},{6,7},{7,8},{8,9},{9,10},{10,1... | collective-permute-start | bytes 393224 | tf_op jit(solution)/shard_map/while/body/eval_jaxpr/ppermute | solution.py:12
  167.9 13.3 %collective-permute-start = (bf16[1,512,128]{2,1,0:T(8,128)(2,1)S(1)}, bf16[1,512,128]{2,1,0:T(8,128)(2,1)S(1)}, u32[]{:S(2)}, u32[]{:S(2)}) collective-permute-start(bf16[1,512,128]{2,1,0:T(8,128)(2,1)S(1)} %get-tuple-element.595), channel_id=1, source_target_pairs={{32,0},{64,32},{96,64},{128,96},{160,128},{192,160},{224,192},{33,... | collective-permute-start | bytes 393224 | tf_op jit(solution)/shard_map/while/body/eval_jaxpr/ppermute | solution.py:12
  169.2 14.5 %collective-permute-start.1 = (bf16[1,512,128]{2,1,0:T(8,128)(2,1)S(1)}, bf16[1,512,128]{2,1,0:T(8,128)(2,1)S(1)}, u32[]{:S(2)}, u32[]{:S(2)}) collective-permute-start(bf16[1,512,128]{2,1,0:T(8,128)(2,1)S(1)} %get-tuple-element.596), channel_id=1, source_target_pairs={{0,1},{1,2},{2,3},{3,4},{4,5},{5,6},{6,7},{7,8},{8,9},{9,10},{10,1... | collective-permute-start | bytes 393224 | tf_op jit(solution)/shard_map/while/body/eval_jaxpr/ppermute | solution.py:12
  184.6 12.5 %collective-permute-start = (bf16[1,512,128]{2,1,0:T(8,128)(2,1)S(1)}, bf16[1,512,128]{2,1,0:T(8,128)(2,1)S(1)}, u32[]{:S(2)}, u32[]{:S(2)}) collective-permute-start(bf16[1,512,128]{2,1,0:T(8,128)(2,1)S(1)} %get-tuple-element.595), channel_id=1, source_target_pairs={{32,0},{64,32},{96,64},{128,96},{160,128},{192,160},{224,192},{33,... | collective-permute-start | bytes 393224 | tf_op jit(solution)/shard_map/while/body/eval_jaxpr/ppermute | solution.py:12
  185.9 13.7 %collective-permute-start.1 = (bf16[1,512,128]{2,1,0:T(8,128)(2,1)S(1)}, bf16[1,512,128]{2,1,0:T(8,128)(2,1)S(1)}, u32[]{:S(2)}, u32[]{:S(2)}) collective-permute-start(bf16[1,512,128]{2,1,0:T(8,128)(2,1)S(1)} %get-tuple-element.596), channel_id=1, source_target_pairs={{0,1},{1,2},{2,3},{3,4},{4,5},{5,6},{6,7},{7,8},{8,9},{9,10},{10,1... | collective-permute-start | bytes 393224 | tf_op jit(solution)/shard_map/while/body/eval_jaxpr/ppermute | solution.py:12
  224.8 13.4 %collective-permute-start = (bf16[1,512,128]{2,1,0:T(8,128)(2,1)S(1)}, bf16[1,512,128]{2,1,0:T(8,128)(2,1)S(1)}, u32[]{:S(2)}, u32[]{:S(2)}) collective-permute-start(bf16[1,512,128]{2,1,0:T(8,128)(2,1)S(1)} %get-tuple-element.595), channel_id=1, source_target_pairs={{32,0},{64,32},{96,64},{128,96},{160,128},{192,160},{224,192},{33,... | collective-permute-start | bytes 393224 | tf_op jit(solution)/shard_map/while/body/eval_jaxpr/ppermute | solution.py:12
  226.1 14.0 %collective-permute-start.1 = (bf16[1,512,128]{2,1,0:T(8,128)(2,1)S(1)}, bf16[1,512,128]{2,1,0:T(8,128)(2,1)S(1)}, u32[]{:S(2)}, u32[]{:S(2)}) collective-permute-start(bf16[1,512,128]{2,1,0:T(8,128)(2,1)S(1)} %get-tuple-element.596), channel_id=1, source_target_pairs={{0,1},{1,2},{2,3},{3,4},{4,5},{5,6},{6,7},{7,8},{8,9},{9,10},{10,1... | collective-permute-start | bytes 393224 | tf_op jit(solution)/shard_map/while/body/eval_jaxpr/ppermute | solution.py:12
  241.1 13.2 %collective-permute-start = (bf16[1,512,128]{2,1,0:T(8,128)(2,1)S(1)}, bf16[1,512,128]{2,1,0:T(8,128)(2,1)S(1)}, u32[]{:S(2)}, u32[]{:S(2)}) collective-permute-start(bf16[1,512,128]{2,1,0:T(8,128)(2,1)S(1)} %get-tuple-element.595), channel_id=1, source_target_pairs={{32,0},{64,32},{96,64},{128,96},{160,128},{192,160},{224,192},{33,... | collective-permute-start | bytes 393224 | tf_op jit(solution)/shard_map/while/body/eval_jaxpr/ppermute | solution.py:12
  242.4 13.8 %collective-permute-start.1 = (bf16[1,512,128]{2,1,0:T(8,128)(2,1)S(1)}, bf16[1,512,128]{2,1,0:T(8,128)(2,1)S(1)}, u32[]{:S(2)}, u32[]{:S(2)}) collective-permute-start(bf16[1,512,128]{2,1,0:T(8,128)(2,1)S(1)} %get-tuple-element.596), channel_id=1, source_target_pairs={{0,1},{1,2},{2,3},{3,4},{4,5},{5,6},{6,7},{7,8},{8,9},{9,10},{10,1... | collective-permute-start | bytes 393224 | tf_op jit(solution)/shard_map/while/body/eval_jaxpr/ppermute | solution.py:12
  295.7 9.4 collective-permute-start.1
  306.0 13.2 %collective-permute-start = (bf16[1,512,128]{2,1,0:T(8,128)(2,1)S(1)}, bf16[1,512,128]{2,1,0:T(8,128)(2,1)S(1)}, u32[]{:S(2)}, u32[]{:S(2)}) collective-permute-start(bf16[1,512,128]{2,1,0:T(8,128)(2,1)S(1)} %get-tuple-element.595), channel_id=1, source_target_pairs={{32,0},{64,32},{96,64},{128,96},{160,128},{192,160},{224,192},{33,... | collective-permute-start | bytes 393224 | tf_op jit(solution)/shard_map/while/body/eval_jaxpr/ppermute | solution.py:12
  307.3 13.8 %collective-permute-start.1 = (bf16[1,512,128]{2,1,0:T(8,128)(2,1)S(1)}, bf16[1,512,128]{2,1,0:T(8,128)(2,1)S(1)}, u32[]{:S(2)}, u32[]{:S(2)}) collective-permute-start(bf16[1,512,128]{2,1,0:T(8,128)(2,1)S(1)} %get-tuple-element.596), channel_id=1, source_target_pairs={{0,1},{1,2},{2,3},{3,4},{4,5},{5,6},{6,7},{7,8},{8,9},{9,10},{10,1... | collective-permute-start | bytes 393224 | tf_op jit(solution)/shard_map/while/body/eval_jaxpr/ppermute | solution.py:12
  371.1 13.0 %collective-permute-start = (bf16[1,512,128]{2,1,0:T(8,128)(2,1)S(1)}, bf16[1,512,128]{2,1,0:T(8,128)(2,1)S(1)}, u32[]{:S(2)}, u32[]{:S(2)}) collective-permute-start(bf16[1,512,128]{2,1,0:T(8,128)(2,1)S(1)} %get-tuple-element.595), channel_id=1, source_target_pairs={{32,0},{64,32},{96,64},{128,96},{160,128},{192,160},{224,192},{33,... | collective-permute-start | bytes 393224 | tf_op jit(solution)/shard_map/while/body/eval_jaxpr/ppermute | solution.py:12
  372.4 13.6 %collective-permute-start.1 = (bf16[1,512,128]{2,1,0:T(8,128)(2,1)S(1)}, bf16[1,512,128]{2,1,0:T(8,128)(2,1)S(1)}, u32[]{:S(2)}, u32[]{:S(2)}) collective-permute-start(bf16[1,512,128]{2,1,0:T(8,128)(2,1)S(1)} %get-tuple-element.596), channel_id=1, source_target_pairs={{0,1},{1,2},{2,3},{3,4},{4,5},{5,6},{6,7},{7,8},{8,9},{9,10},{10,1... | collective-permute-start | bytes 393224 | tf_op jit(solution)/shard_map/while/body/eval_jaxpr/ppermute | solution.py:12
  387.0 9.1 collective-permute-start
  388.3 9.2 collective-permute-start.1
  427.3 16.1 %collective-permute-start = (bf16[1,512,128]{2,1,0:T(8,128)(2,1)S(1)}, bf16[1,512,128]{2,1,0:T(8,128)(2,1)S(1)}, u32[]{:S(2)}, u32[]{:S(2)}) collective-permute-start(bf16[1,512,128]{2,1,0:T(8,128)(2,1)S(1)} %get-tuple-element.595), channel_id=1, source_target_pairs={{32,0},{64,32},{96,64},{128,96},{160,128},{192,160},{224,192},{33,... | collective-permute-start | bytes 393224 | tf_op jit(solution)/shard_map/while/body/eval_jaxpr/ppermute | solution.py:12
  428.6 16.1 %collective-permute-start.1 = (bf16[1,512,128]{2,1,0:T(8,128)(2,1)S(1)}, bf16[1,512,128]{2,1,0:T(8,128)(2,1)S(1)}, u32[]{:S(2)}, u32[]{:S(2)}) collective-permute-start(bf16[1,512,128]{2,1,0:T(8,128)(2,1)S(1)} %get-tuple-element.596), channel_id=1, source_target_pairs={{0,1},{1,2},{2,3},{3,4},{4,5},{5,6},{6,7},{7,8},{8,9},{9,10},{10,1... | collective-permute-start | bytes 393224 | tf_op jit(solution)/shard_map/while/body/eval_jaxpr/ppermute | solution.py:12
  445.7 13.5 %collective-permute-start = (bf16[1,512,128]{2,1,0:T(8,128)(2,1)S(1)}, bf16[1,512,128]{2,1,0:T(8,128)(2,1)S(1)}, u32[]{:S(2)}, u32[]{:S(2)}) collective-permute-start(bf16[1,512,128]{2,1,0:T(8,128)(2,1)S(1)} %get-tuple-element.595), channel_id=1, source_target_pairs={{32,0},{64,32},{96,64},{128,96},{160,128},{192,160},{224,192},{33,... | collective-permute-start | bytes 393224 | tf_op jit(solution)/shard_map/while/body/eval_jaxpr/ppermute | solution.py:12
  447.0 14.1 %collective-permute-start.1 = (bf16[1,512,128]{2,1,0:T(8,128)(2,1)S(1)}, bf16[1,512,128]{2,1,0:T(8,128)(2,1)S(1)}, u32[]{:S(2)}, u32[]{:S(2)}) collective-permute-start(bf16[1,512,128]{2,1,0:T(8,128)(2,1)S(1)} %get-tuple-element.596), channel_id=1, source_target_pairs={{0,1},{1,2},{2,3},{3,4},{4,5},{5,6},{6,7},{7,8},{8,9},{9,10},{10,1... | collective-permute-start | bytes 393224 | tf_op jit(solution)/shard_map/while/body/eval_jaxpr/ppermute | solution.py:12
  462.1 10.4 %collective-permute-start = (bf16[1,512,128]{2,1,0:T(8,128)(2,1)S(1)}, bf16[1,512,128]{2,1,0:T(8,128)(2,1)S(1)}, u32[]{:S(2)}, u32[]{:S(2)}) collective-permute-start(bf16[1,512,128]{2,1,0:T(8,128)(2,1)S(1)} %get-tuple-element.595), channel_id=1, source_target_pairs={{32,0},{64,32},{96,64},{128,96},{160,128},{192,160},{224,192},{33,... | collective-permute-start | bytes 393224 | tf_op jit(solution)/shard_map/while/body/eval_jaxpr/ppermute | solution.py:12
  463.4 10.4 %collective-permute-start.1 = (bf16[1,512,128]{2,1,0:T(8,128)(2,1)S(1)}, bf16[1,512,128]{2,1,0:T(8,128)(2,1)S(1)}, u32[]{:S(2)}, u32[]{:S(2)}) collective-permute-start(bf16[1,512,128]{2,1,0:T(8,128)(2,1)S(1)} %get-tuple-element.596), channel_id=1, source_target_pairs={{0,1},{1,2},{2,3},{3,4},{4,5},{5,6},{6,7},{7,8},{8,9},{9,10},{10,1... | collective-permute-start | bytes 393224 | tf_op jit(solution)/shard_map/while/body/eval_jaxpr/ppermute | solution.py:12
  476.1 9.0 collective-permute-start.1
  487.4 9.0 collective-permute-start.1
  498.7 9.0 collective-permute-start.1
  510.0 9.0 collective-permute-start.1
  521.3 9.0 collective-permute-start.1
  532.7 9.0 collective-permute-start.1
  544.0 9.0 collective-permute-start.1
  555.3 9.0 collective-permute-start.1
  566.6 9.0 collective-permute-start.1
  589.2 9.0 collective-permute-start.1
  657.0 9.0 collective-permute-start.1
  736.1 9.0 collective-permute-start.1
  804.0 9.0 collective-permute-start.1
  871.8 9.0 collective-permute-start.1
  916.3 122.1 %all-to-all-start = ((f32[32,1,512]{2,1,0:T(1,128)}), f32[32,1,512]{2,1,0:T(1,128)S(1)}, u32[]{:S(2)}, u32[]{:S(2)}) async-start(f32[32,1,512]{2,1,0:T(1,128)} %broadcast_in_dim.7), calls=%async_computation | async-start | bytes 131072 | tf_op jit(solution)/shard_map/all_to_all | solution.py:17
  (107 other events, 881.5 us)
where the time goes:
time: 1050 us; the launch traced here: 1040 us
  starting transfers between devices  709 us (68%)
  local copies, waits for them, and re-layouts  158 us (15%)
  waiting for transfers between devices  132 us (13%)
  matrix products  17 us (2%)
  blocking collectives  12 us (1%)
    ppermute x154, starting transfers between devices, shifted(): lax.ppermute(value, axis, [(source, source + steps) for source in range(l...  600 us
    ppermute x154, waiting for transfers between devices, shifted(): lax.ppermute(value, axis, [(source, source + steps) for source in range(l...  132 us
    all_to_all x1, starting transfers between devices, copy_for_each(): return lax.all_to_all(copies, axis, split_axis=0, concat_axis=0, tiled=True)  109 us
    another operation x79, local copies, waits for them, and re-layouts  83.6 us
    cond x76, local copies, waits for them, and re-layouts, advance(): lax.cond(row_valid, lambda operands: lower_update(operands[0], operands[1...  62.3 us
  transfers between devices with their start and end apart: 155, of which 142 were waited for; matrix products, arithmetic and copies ran while one was open for 9% of the time, Pallas kernels for 0%

commit v1 on v0

v1 whole, which is shorter than its diff:
```python
import functools

import jax
import jax.numpy as jnp
from jax import lax
from jax.experimental import pallas as pl
from jax.experimental.pallas import tpu as pltpu
from jax.sharding import PartitionSpec as P

MESH = pl.DeviceIdType.MESH
GROUP = 8
SOLVER = 1
HELPER = 0
TERMS = 4
F32 = jnp.float32
BF16 = jnp.bfloat16


def dot(left, right):
    return jnp.dot(left, right, preferred_element_type=F32)


def kernel(
    n_row, n_col,
    signs_ref, a_ref, b_ref, d_ref,
    out_ref, norm_ref, peak_ref,
    powers, couple, series, strip, solved, below, partial, passed, total, residual,
    stage, peaks, norm_all, peak_all, final_out,
    total_own, lower, own, partial_out, series_out, sign_out, sign_in, final_in,
    near_send, near_recv, far_send, far_recv, series_send, series_recv,
    sign_send, sign_recv, partial_send, partial_recv, below_send, below_recv,
    passed_send, passed_recv, relay_send, own_send, own_recv, lower_send, lower_recv,
    skip_send, norm_send, norm_recv, peak_send, peak_recv, final_send, final_recv,
):
    r = lax.axis_index("row")
    c = lax.axis_index("col")
    g = c // GROUP
    pos = c % GROUP
    first = g * GROUP
    n_group = n_col // GROUP
    bc = b_ref.shape[1]
    br = d_ref.shape[0]
    wide = GROUP * bc
    is_solver = pos == SOLVER
    is_helper = pos != SOLVER
    has_extra = pos == HELPER
    last_row = n_row - 1
    last_group = n_group - 1
    barrier = pltpu.get_barrier_semaphore()

    def remote(src, dst, send, recv, row, col):
        return pltpu.make_async_remote_copy(
            src_ref=src, dst_ref=dst, send_sem=send, recv_sem=recv,
            device_id=(row, col), device_id_type=MESH,
        )

    def greet(row, col):
        pl.semaphore_signal(barrier, inc=1, device_id=(row, col), device_id_type=MESH)

    def cols(index):
        return pl.ds(pl.multiple_of(index * bc, bc), bc)

    def rows(index, size):
        return pl.ds(pl.multiple_of(index * size, size), size)

    @pl.when(is_solver)
    def _():
        couple[rows(g, wide), :] = jnp.zeros((wide, wide), BF16)
        for p in range(GROUP):
            if p != SOLVER:
                greet(r, first + p)
        for step in range(1, n_row):
            greet((r + step) % n_row, c)
        for step in range(1, n_group):
            greet(r, (c + step * GROUP) % n_col)

        sign_out[...] = (2 * signs_ref[...] - 1).astype(BF16)
        strip[...] = jnp.zeros(strip.shape, BF16)
        total[...] = jnp.zeros(total.shape, F32)
        peaks[...] = jnp.zeros(peaks.shape, F32)
        diag = d_ref[...]
        second = dot(diag, diag).astype(BF16)
        powers[:, 0:br] = diag
        powers[:, br:2 * br] = second
        powers[:, 2 * br:3 * br] = dot(second, diag).astype(BF16)
        powers[:, 3 * br:4 * br] = dot(second, second).astype(BF16)
        mine = b_ref[cols(c), :]
        square = dot(mine, mine).astype(BF16)
        series[SOLVER, :, 0:bc] = -mine
        series[SOLVER, :, bc:2 * bc] = square
        series[SOLVER, :, 2 * bc:3 * bc] = (-dot(square, mine)).astype(BF16)
        for kb in range(SOLVER):
            couple[cols(first + kb), SOLVER * bc:(SOLVER + 1) * bc] = b_ref[cols(first + kb), :]
        for block in range(last_group):
            @pl.when(block < g)
            def _():
                couple[block * wide:(block + 1) * wide, SOLVER * bc:(SOLVER + 1) * bc] = b_ref[block * wide:(block + 1) * wide, :]

        pl.semaphore_wait(barrier, GROUP - 1 + n_row - 1 + n_group - 1)
        sign_copy = remote(sign_out, sign_in, sign_send, sign_recv, r, first + HELPER)
        sign_copy.start()

        def pass_on(k):
            return remote(passed.at[k], passed.at[k], relay_send.at[k], passed_recv.at[k], r, c + GROUP)

        for block in range(last_group):
            @pl.when(block < g)
            def _():
                for j in range(GROUP):
                    if j != SOLVER:
                        remote(
                            b_ref.at[pl.ds(block * wide, wide), :],
                            couple.at[pl.ds(block * wide, wide), pl.ds(j * bc, bc)],
                            far_send.at[block], far_recv.at[j, block], r, first + j,
                        ).wait_recv()

                def take(i, carry):
                    k = block * GROUP + i
                    remote(passed.at[k], passed.at[k], relay_send.at[k], passed_recv.at[k], r, (c + n_col - GROUP) % n_col).wait_recv()

                    @pl.when(g < last_group)
                    def _():
                        pass_on(k).start()

                    total[...] -= dot(passed[k], couple[cols(k), :])
                    return carry

                lax.fori_loop(0, GROUP, take, 0)

        def send_up(j):
            return remote(solved.at[j], below.at[j], below_send.at[j], below_recv.at[j], (r + n_row - 1) % n_row, c)

        def send_right(j):
            return remote(solved.at[j], passed.at[first + j], passed_send.at[j], passed_recv.at[first + j], r, (c + GROUP) % n_col)

        def send_own(j):
            return remote(solved.at[j], own.at[1], own_send.at[j], own_recv.at[1], r, first + j)

        def send_extra(j):
            return remote(solved.at[j], own.at[0], own_send.at[j], own_recv.at[0], r, first + HELPER)

        def column(j, carry):
            @pl.when(j != SOLVER)
            def _():
                remote(series_out, series.at[j], series_send, series_recv.at[j], r, first + j).wait_recv()
                for kb in range(GROUP - 1):
                    @pl.when(kb < j)
                    def _():
                        remote(
                            b_ref.at[cols(first + kb), :], couple.at[cols(first + kb), cols(j)],
                            near_send.at[kb], near_recv.at[j, kb], r, first + j,
                        ).wait_recv()

            near = dot(strip[...], couple[rows(g, wide), cols(j)])
            residual[...] = total[:, cols(j)] - near
            remote(partial_out.at[0], partial.at[j], partial_send.at[0], partial_recv.at[j], r, first + HELPER).wait_recv()
            residual[...] += partial[j].astype(F32)

            @pl.when(r < last_row)
            def _():
                send_down = remote(solved.at[j], below.at[j], below_send.at[j], below_recv.at[j], (r + 1) % n_row, c)
                send_down.wait_recv()
                residual[...] -= dot(a_ref[:, rows(r + 1, br)], below[j])

            lead = residual[...].astype(BF16)
            rest = dot(lead, series[j]).astype(BF16)
            stage[0:br, :] = lead
            for m in range(1, TERMS):
                stage[m * br:(m + 1) * br, :] = rest[:, (m - 1) * bc:m * bc]
            value = dot(powers[...], stage[...]).astype(BF16)
            solved[j] = value

            @pl.when(r > 0)
            def _():
                send_up(j).start()

            @pl.when(g < last_group)
            def _():
                send_right(j).start()

            @pl.when(j != SOLVER)
            def _():
                send_own(j).start()

            @pl.when(j == SOLVER)
            def _():
                send_extra(j).start()

            strip[:, cols(j)] = value
            magnitude = jnp.abs(value.astype(F32))
            peaks[...] = jnp.maximum(peaks[...], magnitude)
            norm_all[r, pl.ds(j, 1), :] = jnp.sum(magnitude, axis=0, keepdims=True)
            return carry

        lax.fori_loop(0, GROUP, column, 0)

        peak_all[g] = jnp.max(jnp.transpose(peaks[...]), axis=0, keepdims=True)
        for step in range(1, n_row):
            remote(norm_all.at[r], norm_all.at[r], norm_send.at[step - 1], norm_recv.at[r], (r + step) % n_row, c).start()
        for step in range(1, n_group):
            remote(peak_all.at[g], peak_all.at[g], peak_send.at[step - 1], peak_recv.at[g], r, (c + step * GROUP) % n_col).start()
        out_ref[...] = solved[SOLVER]
        for step in range(1, n_row):
            source = (r + step) % n_row
            remote(norm_all.at[source], norm_all.at[source], norm_send.at[step - 1], norm_recv.at[source], source, c).wait_recv()
        for step in range(1, n_group):
            source = (g + step) % n_group
            remote(peak_all.at[source], peak_all.at[source], peak_send.at[step - 1], peak_recv.at[source], r, source * GROUP + SOLVER).wait_recv()
        norms = norm_all[0]
        for source in range(1, n_row):
            norms = norms + norm_all[source]
        top = peak_all[0]
        for source in range(1, n_group):
            top = jnp.maximum(top, peak_all[source])
        for j in range(GROUP):
            final_out[j, :, 0:bc] = norms[j:j + 1, :]
            final_out[j, :, bc:bc + br] = top
        for j in range(GROUP):
            if j != SOLVER:
                remote(final_out.at[j], final_in, final_send.at[j], final_recv, r, first + j).start()
        norm_ref[...] = norms[SOLVER:SOLVER + 1, :]
        peak_ref[...] = top

        sign_copy.wait_send()
        for block in range(last_group):
            @pl.when((block < g) & (g < last_group))
            def _():
                def drain(i, carry):
                    pass_on(block * GROUP + i).wait_send()
                    return carry

                lax.fori_loop(0, GROUP, drain, 0)

        def finish(j, carry):
            @pl.when(r > 0)
            def _():
                send_up(j).wait_send()

            @pl.when(g < last_group)
            def _():
                send_right(j).wait_send()

            send_extra(j).wait_send()
            return carry

        lax.fori_loop(0, GROUP, finish, 0)
        for step in range(1, n_row):
            remote(norm_all.at[r], norm_all.at[r], norm_send.at[step - 1], norm_recv.at[r], (r + step) % n_row, c).wait_send()
        for step in range(1, n_group):
            remote(peak_all.at[g], peak_all.at[g], peak_send.at[step - 1], peak_recv.at[g], r, (c + step * GROUP) % n_col).wait_send()
        for j in range(GROUP):
            if j != SOLVER:
                remote(final_out.at[j], final_in, final_send.at[j], final_recv, r, first + j).wait_send()

    @pl.when(is_helper)
    def _():
        solver = first + SOLVER
        greet(r, solver)
        for step in (1, 2, n_row - 2, n_row - 1):
            greet((r + step) % n_row, c)
        mine = b_ref[cols(c), :]
        square = dot(mine, mine).astype(BF16)
        series_out[:, 0:bc] = -mine
        series_out[:, bc:2 * bc] = square
        series_out[:, 2 * bc:3 * bc] = (-dot(square, mine)).astype(BF16)
        total_own[1] = (2 * signs_ref[...] - 1).astype(F32)
        pl.semaphore_wait(barrier, 5)

        series_copy = remote(series_out, series.at[pos], series_send, series_recv.at[pos], r, solver)
        series_copy.start()

        def near_copy(kb):
            return remote(
                b_ref.at[cols(first + kb), :], couple.at[cols(first + kb), cols(pos)],
                near_send.at[kb], near_recv.at[pos, kb], r, solver,
            )

        def far_copy(block):
            return remote(
                b_ref.at[pl.ds(block * wide, wide), :],
                couple.at[pl.ds(block * wide, wide), cols(pos)],
                far_send.at[block], far_recv.at[pos, block], r, solver,
            )

        for kb in range(GROUP - 1):
            @pl.when(kb < pos)
            def _():
                near_copy(kb).start()
        for block in range(last_group):
            @pl.when(block < g)
            def _():
                far_copy(block).start()

        @pl.when(has_extra)
        def _():
            remote(sign_out, sign_in, sign_send, sign_recv, r, solver).wait_recv()
            total_own[0] = sign_in[...].astype(F32)

        def relay(slot, k):
            return remote(lower.at[slot, k], lower.at[slot, k], lower_send.at[slot, k], lower_recv.at[slot, k], (r + n_row - 1) % n_row, c)

        def apply(slot, k):
            remote(lower.at[slot, k], lower.at[slot, k], lower_send.at[slot, k], lower_recv.at[slot, k], (r + 1) % n_row, c).wait_recv()

            @pl.when(r > 0)
            def _():
                relay(slot, k).start()

            total_own[slot] -= dot(a_ref[:, rows(k, br)], lower[slot, k])

        def sweep(i, carry):
            k = last_row - i

            @pl.when(k >= r + 2)
            def _():
                apply(1, k)

                @pl.when(has_extra)
                def _():
                    apply(0, k)

            return carry

        lax.fori_loop(0, n_row - 2, sweep, 0)

        def give(slot, j):
            return remote(partial_out.at[slot], partial.at[j], partial_send.at[slot], partial_recv.at[j], r, solver)

        def skip(slot):
            return remote(own.at[slot], lower.at[slot, r], skip_send.at[slot], lower_recv.at[slot, r], (r + n_row - 2) % n_row, c)

        partial_out[1] = total_own[1].astype(BF16)
        give(1, pos).start()

        @pl.when(has_extra)
        def _():
            partial_out[0] = total_own[0].astype(BF16)
            give(0, SOLVER).start()

        remote(own.at[1], own.at[1], skip_send.at[1], own_recv.at[1], r, solver).wait_recv()

        @pl.when(r > 1)
        def _():
            skip(1).start()

        @pl.when(has_extra)
        def _():
            remote(own.at[0], own.at[0], skip_send.at[0], own_recv.at[0], r, solver).wait_recv()

            @pl.when(r > 1)
            def _():
                skip(0).start()

        out_ref[...] = own[1]

        series_copy.wait_send()
        for kb in range(GROUP - 1):
            @pl.when(kb < pos)
            def _():
                near_copy(kb).wait_send()
        for block in range(last_group):
            @pl.when(block < g)
            def _():
                far_copy(block).wait_send()
        give(1, pos).wait_send()

        @pl.when(has_extra)
        def _():
            give(0, SOLVER).wait_send()

        def settle(i, carry):
            k = last_row - i

            @pl.when((k >= r + 2) & (r > 0))
            def _():
                relay(1, k).wait_send()

                @pl.when(has_extra)
                def _():
                    relay(0, k).wait_send()

            return carry

        lax.fori_loop(0, n_row - 2, settle, 0)

        @pl.when(r > 1)
        def _():
            skip(1).wait_send()

            @pl.when(has_extra)
            def _():
                skip(0).wait_send()

        remote(final_in, final_in, final_send.at[0], final_recv, r, solver).wait_recv()
        norm_ref[...] = final_in[:, 0:bc]
        peak_ref[...] = final_in[:, bc:bc + br]


def solution(mesh):
    n_row = mesh.shape["row"]
    n_col = mesh.shape["col"]

    def shards(signs, upper_a, upper_b, diag_inverse):
        br = diag_inverse.shape[0]
        bc = upper_b.shape[1]
        order = upper_b.shape[0]
        wide = GROUP * bc
        n_group = n_col // GROUP
        dma = pltpu.SemaphoreType.DMA
        solved, norms, peaks = pl.pallas_call(
            functools.partial(kernel, n_row, n_col),
            out_shape=(
                jax.ShapeDtypeStruct((br, bc), BF16),
                jax.ShapeDtypeStruct((1, bc), F32),
                jax.ShapeDtypeStruct((1, br), F32),
            ),
            in_specs=[pl.BlockSpec(memory_space=pltpu.VMEM)] * 4,
            out_specs=[pl.BlockSpec(memory_space=pltpu.VMEM)] * 3,
            scratch_shapes=[
                pltpu.VMEM((br, TERMS * br), BF16),
                pltpu.VMEM((order, wide), BF16),
                pltpu.VMEM((GROUP, bc, (TERMS - 1) * bc), BF16),
                pltpu.VMEM((br, wide), BF16),
                pltpu.VMEM((GROUP, br, bc), BF16),
                pltpu.VMEM((GROUP, br, bc), BF16),
                pltpu.VMEM((GROUP, br, bc), BF16),
                pltpu.VMEM((n_col, br, bc), BF16),
                pltpu.VMEM((br, wide), F32),
                pltpu.VMEM((br, bc), F32),
                pltpu.VMEM((TERMS * br, bc), BF16),
                pltpu.VMEM((br, bc), F32),
                pltpu.VMEM((n_row, GROUP, bc), F32),
                pltpu.VMEM((n_group, 1, br), F32),
                pltpu.VMEM((GROUP, 1, bc + br), F32),
                pltpu.VMEM((2, br, bc), F32),
                pltpu.VMEM((2, n_row, br, bc), BF16),
                pltpu.VMEM((2, br, bc), BF16),
                pltpu.VMEM((2, br, bc), BF16),
                pltpu.VMEM((bc, (TERMS - 1) * bc), BF16),
                pltpu.VMEM((br, bc), BF16),
                pltpu.VMEM((br, bc), BF16),
                pltpu.VMEM((1, bc + br), F32),
                dma((GROUP,)), dma((GROUP, GROUP)),
                dma((n_group,)), dma((GROUP, n_group)),
                dma, dma((GROUP,)),
                dma, dma,
                dma((2,)), dma((GROUP,)),
                dma((GROUP,)), dma((GROUP,)),
                dma((GROUP,)), dma((n_col,)),
                dma((n_col,)),
                dma((GROUP,)), dma((2,)),
                dma((2, n_row)), dma((2, n_row)),
                dma((2,)),
                dma((n_row,)), dma((n_row,)),
                dma((n_group,)), dma((n_group,)),
                dma((GROUP,)), dma,
            ],
            compiler_params=pltpu.CompilerParams(
                collective_id=0, has_side_effects=True, vmem_limit_bytes=60 * 1024 * 1024
            ),
        )(signs[0], upper_a, upper_b, diag_inverse)
        return solved[None], norms, peaks

    in_specs = (P(None, "row", "col"), P("row", None), P(None, "col"), P("row", None))
    out_specs = (P(None, "row", "col"), P(None, "col"), P(None, "row"))
    return jax.shard_map(shards, mesh=mesh, in_specs=in_specs, out_specs=out_specs, check_vma=False)
```

time: 1050 us -> 172 us (0.16); the launches traced: 1040 us -> 172 us
  starting transfers between devices: 709 us -> 0 us
  Pallas kernels: 0 us -> 167 us
  local copies, waits for them, and re-layouts: 158 us -> 3.99 us
  waiting for transfers between devices: 132 us -> 0 us
  matrix products: 17 us -> 0 us
  blocking collectives: 12 us -> 0 us
    ppermute x154 -> x0, starting transfers between devices: 600 us -> none  [shifted(): lax.ppermute(value, axis, [(source, source + steps) for source in range(l...]
    pallas_call x0 -> x1, Pallas kernels: none -> 167 us  [shards(): pl.pallas_call(functools.partial(kernel, n_row, n_col), out_shape=(jax.Sh...]
    ppermute x154 -> x0, waiting for transfers between devices: 132 us -> none  [shifted(): lax.ppermute(value, axis, [(source, source + steps) for source in range(l...]
    all_to_all x1 -> x0, starting transfers between devices: 109 us -> none  [copy_for_each(): return lax.all_to_all(copies, axis, split_axis=0, concat_axis=0, tiled=True)]
    another operation x79 -> x0, local copies, waits for them, and re-layouts: 83.6 us -> none
    cond x153 -> x0, local copies, waits for them, and re-layouts: 71.2 us -> none  [the longest x76 62.3 us: advance(): lax.cond(row_valid, lambda operands: lower_update(operands[0], operands[1...]
    dot_general x12 -> x0, matrix products: 17 us -> none  [the longest x7 9.38 us: lower_update(): jnp.einsum('ij,pjk->pik', coupling, tile, preferred_element_type=jnp.floa...]
    psum x1 -> x0, blocking collectives: 12 us -> none  [shards(): col_total = lax.psum(jnp.sum(magnitude, axis=1), 'row')]
  transfers between devices with their start and end apart: 155 -> 0, of which waited for: 142 -> 0; matrix products, arithmetic and copies ran while one was open for 9% -> 0% of each run, Pallas kernels for 0% -> 0%
where the time goes in v1:
time: 172 us
  Pallas kernels  167 us (97%)
  local copies, waits for them, and re-layouts  3.99 us (2%)
    pallas_call x1, Pallas kernels, shards(): pl.pallas_call(functools.partial(kernel, n_row, n_col), out_shape=(jax.Sh...  167 us
    unnamed x3, local copies, waits for them, and re-layouts  3.99 us

profile of v1, /device:TPU:1, one launch (start us, length us, event | category | flops | bytes accessed | tf_op | source)
XLA Modules:
  0.0 172.0 jit_solution(18403781309218095946)
XLA Ops:
  0.6 167.3 %shard_map.67 = (bf16[512,128]{1,0:T(8,128)(2,1)}, f32[1,128]{1,0:T(1,128)}, f32[1,512]{1,0:T(1,128)}) custom-call(s32[512,128]{1,0:T(8,128)} %bitcast.2, bf16[512,4096]{1,0:T(8,128)(2,1)} %a_ref.1, bf16[4096,128]{1,0:T(8,128)(2,1)} %b_ref.1, bf16[512,512]{1,0:T(8,128)(2,1)} %d_ref.1), custom_call_target="tpu_custom_call" | custom-call | tf_op jit(solution)/shard_map/pallas_call | solution.py:410
  168.0 1.6 copy.10
  169.6 1.2 copy.11
  170.7 1.3 copy.12

commit v2 on v1

v2 whole, which is shorter than its diff:
```python
import functools

import jax
import jax.numpy as jnp
from jax import lax
from jax.experimental import pallas as pl
from jax.experimental.pallas import tpu as pltpu
from jax.sharding import PartitionSpec as P

MESH = pl.DeviceIdType.MESH
GROUP = 8
SOLVER = 1
SIDE = 0
PASS_FROM = 4
PASS_TO = 2
DOWN = 3
PARTS = 2
TERMS = 4
F32 = jnp.float32
BF16 = jnp.bfloat16


def dot(left, right):
    return jnp.dot(left, right, preferred_element_type=F32)


def kernel(
    n_row, n_col,
    signs_ref, a_ref, b_ref, d_ref,
    out_ref, norm_ref, peak_ref,
    powers, couple, series, strip, solved, below, partial, passed, total, residual,
    stage, peaks, norm_all, peak_all, final_out, next_a,
    total_own, lower, own, partial_out, sign_out, sign_in, final_in, all_a, bounce_near, bounce_far,
    near_send, near_recv, far_send, far_recv, copy_a,
    sign_send, sign_recv, partial_send, partial_recv, below_send, below_recv,
    passed_send, passed_recv, relay_send, own_send, own_recv, extra_send, down_send, up_send, lower_recv,
    skip_send, wrap_send, forward_send, bounce_send, bounce_recv, pass_send, norm_send, norm_recv, peak_send, peak_recv, final_send, final_recv,
):
    r = lax.axis_index("row")
    c = lax.axis_index("col")
    g = c // GROUP
    pos = c % GROUP
    first = g * GROUP
    n_group = n_col // GROUP
    bc = b_ref.shape[1]
    br = d_ref.shape[0]
    wide = GROUP * bc
    half = GROUP // 2
    chunk = br // PARTS
    last_row = n_row - 1
    last_group = n_group - 1
    solver = first + SOLVER
    barrier = pltpu.get_barrier_semaphore()

    def remote(src, dst, send, recv, row, col):
        return pltpu.make_async_remote_copy(
            src_ref=src, dst_ref=dst, send_sem=send, recv_sem=recv,
            device_id=(row, col), device_id_type=MESH,
        )

    def greet(row, col):
        pl.semaphore_signal(barrier, inc=1, device_id=(row, col), device_id_type=MESH)

    def cols(index):
        return pl.ds(pl.multiple_of(index * bc, bc), bc)

    def piece(h):
        return pl.ds(h * chunk, chunk)

    def rows(index, size):
        return pl.ds(pl.multiple_of(index * size, size), size)

    @pl.when(pos == SOLVER)
    def _():
        couple[rows(g, wide), :] = jnp.zeros((wide, wide), BF16)
        for p in range(GROUP):
            if p != SOLVER:
                greet(r, first + p)
        for step in range(1, n_row):
            greet((r + step) % n_row, c)
        for step in range(1, n_group):
            greet(r, (c + step * GROUP) % n_col)

        def fetch():
            return pltpu.make_async_copy(a_ref.at[:, rows(r + 1, br)], next_a, copy_a)

        @pl.when(r < last_row)
        def _():
            fetch().start()

        sign_out[...] = (2 * signs_ref[...] - 1).astype(BF16)
        strip[...] = jnp.zeros(strip.shape, BF16)
        total[...] = jnp.zeros(total.shape, F32)
        peaks[...] = jnp.zeros(peaks.shape, F32)
        for kb in range(SOLVER + 1):
            couple[cols(first + kb), SOLVER * bc:(SOLVER + 1) * bc] = b_ref[cols(first + kb), :]
        for block in range(last_group):
            @pl.when(block < g)
            def _():
                couple[block * wide:(block + 1) * wide, SOLVER * bc:(SOLVER + 1) * bc] = b_ref[block * wide:(block + 1) * wide, :]

        pl.semaphore_wait(barrier, GROUP - 1 + n_row - 1 + n_group - 1)

        def sign_copy():
            return remote(sign_out, sign_in.at[0], sign_send, sign_recv.at[0], r, first + half - 1)

        @pl.when(r < n_row - 2)
        def _():
            sign_copy().start()

        @pl.when(r >= n_row - 2)
        def _():
            partial[SOLVER] = sign_out[...]

        diag = d_ref[...]
        second = dot(diag, diag).astype(BF16)
        powers[:, 0:br] = diag
        powers[:, br:2 * br] = second
        powers[:, 2 * br:3 * br] = dot(second, diag).astype(BF16)
        powers[:, 3 * br:4 * br] = dot(second, second).astype(BF16)

        def pass_on(k):
            return remote(passed.at[k], passed.at[k], relay_send.at[k], passed_recv.at[k], r, (c + GROUP) % n_col)

        for block in range(last_group):
            @pl.when(block < g)
            def _():
                for j in range(GROUP):
                    if j != SOLVER:
                        remote(
                            b_ref.at[pl.ds(block * wide, wide), :],
                            couple.at[pl.ds(block * wide, wide), pl.ds(j * bc, bc)],
                            far_send.at[block], far_recv.at[j, block], r, first + j,
                        ).wait_recv()

                def take(i, carry):
                    k = block * GROUP + i
                    remote(passed.at[k], passed.at[k], relay_send.at[k], passed_recv.at[k], r, (c + n_col - GROUP) % n_col).wait_recv()

                    @pl.when(g < last_group)
                    def _():
                        pass_on(k).start()

                    total[...] -= dot(passed[k], couple[cols(k), :])
                    return carry

                lax.fori_loop(0, GROUP, take, 0)

        @pl.when(r < last_row)
        def _():
            fetch().wait()

        def send_up(j, h):
            return remote(solved.at[j, piece(h)], below.at[j, piece(h)], below_send.at[j, h], below_recv.at[j, h], (r + n_row - 1) % n_row, c)

        def send_right(j):
            return remote(solved.at[j], passed.at[first + j], passed_send.at[j], passed_recv.at[first + j], r, (c + GROUP) % n_col)

        def send_own(j, h):
            return remote(solved.at[j, piece(h)], own.at[1 + j % 2, piece(h)], own_send.at[j, h], own_recv.at[1 + j % 2, h], r, first + j // 2 * 2 + 1)

        def send_side(h):
            return remote(solved.at[SIDE, piece(h)], own.at[0, piece(h)], own_send.at[SIDE, h], own_recv.at[0, h], r, first)

        def send_extra(j, place, h):
            return remote(solved.at[j, piece(h)], own.at[0, piece(h)], extra_send.at[j, h], own_recv.at[0, h], r, first + place)

        def column(j, carry):
            @pl.when(j != SOLVER)
            def _():
                for kb in range(GROUP):
                    @pl.when(kb <= j)
                    def _():
                        remote(
                            b_ref.at[cols(first + kb), :], couple.at[cols(first + kb), cols(j)],
                            near_send.at[kb], near_recv.at[j, kb], r, first + j,
                        ).wait_recv()

            mine = couple[cols(first + j), cols(j)]
            square = dot(mine, mine).astype(BF16)
            series[:, 0:bc] = -mine
            series[:, bc:2 * bc] = square
            series[:, 2 * bc:3 * bc] = (-dot(square, mine)).astype(BF16)
            near = dot(strip[...], couple[rows(g, wide), cols(j)])
            residual[...] = total[:, cols(j)] - near

            @pl.when((j != SOLVER) | (r < n_row - 2))
            def _():
                remote(partial_out.at[1], partial.at[j], partial_send.at[1], partial_recv.at[j], r, first).wait_recv()

            residual[...] += partial[j].astype(F32)

            @pl.when(r < last_row)
            def _():
                for h in range(PARTS):
                    remote(
                        solved.at[j, piece(h)], below.at[j, piece(h)], below_send.at[j, h], below_recv.at[j, h], (r + 1) % n_row, c,
                    ).wait_recv()
                residual[...] -= dot(next_a[...], below[j])

            lead = residual[...].astype(BF16)
            rest = dot(lead, series[...]).astype(BF16)
            stage[0:br, :] = lead
            for m in range(1, TERMS):
                stage[m * br:(m + 1) * br, :] = rest[:, (m - 1) * bc:m * bc]
            for h in range(PARTS):
                solved[j, piece(h), :] = dot(powers[piece(h), :], stage[...]).astype(BF16)

                @pl.when(r > 0)
                def _():
                    send_up(j, h).start()

                @pl.when(r > 1)
                def _():
                    @pl.when(j == SIDE)
                    def _():
                        send_extra(SIDE, GROUP - 1, h).start()

                    @pl.when(j == SOLVER)
                    def _():
                        send_extra(SOLVER, half - 1, h).start()

                @pl.when(j > SOLVER)
                def _():
                    send_own(j, h).start()

                @pl.when(j == SIDE)
                def _():
                    send_side(h).start()

            @pl.when(g < last_group)
            def _():
                send_right(j).start()

            value = solved[j]
            strip[:, cols(j)] = value
            magnitude = jnp.abs(value.astype(F32))
            peaks[...] = jnp.maximum(peaks[...], magnitude)
            norm_all[r, pl.ds(j, 1), :] = jnp.sum(magnitude, axis=0, keepdims=True)
            return carry

        lax.fori_loop(0, GROUP, column, 0)

        peak_all[g] = jnp.max(jnp.transpose(peaks[...]), axis=0, keepdims=True)
        for step in range(1, n_row):
            remote(norm_all.at[r], norm_all.at[r], norm_send.at[step - 1], norm_recv.at[r], (r + step) % n_row, c).start()
        for step in range(1, n_group):
            remote(peak_all.at[g], peak_all.at[g], peak_send.at[step - 1], peak_recv.at[g], r, (c + step * GROUP) % n_col).start()
        out_ref[...] = solved[SOLVER]
        for step in range(1, n_row):
            source = (r + step) % n_row
            remote(norm_all.at[source], norm_all.at[source], norm_send.at[step - 1], norm_recv.at[source], source, c).wait_recv()
        for step in range(1, n_group):
            source = (g + step) % n_group
            remote(peak_all.at[source], peak_all.at[source], peak_send.at[step - 1], peak_recv.at[source], r, source * GROUP + SOLVER).wait_recv()
        norms = norm_all[0]
        for source in range(1, n_row):
            norms = norms + norm_all[source]
        top = peak_all[0]
        for source in range(1, n_group):
            top = jnp.maximum(top, peak_all[source])
        for j in range(GROUP):
            final_out[j, :, 0:bc] = norms[j:j + 1, :]
            final_out[j, :, bc:bc + br] = top
        for j in range(GROUP):
            if j != SOLVER:
                remote(final_out.at[j], final_in, final_send.at[j], final_recv, r, first + j).start()
        norm_ref[...] = norms[SOLVER:SOLVER + 1, :]
        peak_ref[...] = top

        @pl.when(r < n_row - 2)
        def _():
            sign_copy().wait_send()

        for block in range(last_group):
            @pl.when((block < g) & (g < last_group))
            def _():
                def drain(i, carry):
                    pass_on(block * GROUP + i).wait_send()
                    return carry

                lax.fori_loop(0, GROUP, drain, 0)

        def finish(j, carry):
            @pl.when(r > 0)
            def _():
                for h in range(PARTS):
                    send_up(j, h).wait_send()

            @pl.when(g < last_group)
            def _():
                send_right(j).wait_send()

            @pl.when(j > SOLVER)
            def _():
                for h in range(PARTS):
                    send_own(j, h).wait_send()

            return carry

        lax.fori_loop(0, GROUP, finish, 0)
        for h in range(PARTS):
            send_side(h).wait_send()

        @pl.when(r > 1)
        def _():
            for h in range(PARTS):
                send_extra(SIDE, GROUP - 1, h).wait_send()
                send_extra(SOLVER, half - 1, h).wait_send()

        for step in range(1, n_row):
            remote(norm_all.at[r], norm_all.at[r], norm_send.at[step - 1], norm_recv.at[r], (r + step) % n_row, c).wait_send()
        for step in range(1, n_group):
            remote(peak_all.at[g], peak_all.at[g], peak_send.at[step - 1], peak_recv.at[g], r, (c + step * GROUP) % n_col).wait_send()
        for j in range(GROUP):
            if j != SOLVER:
                remote(final_out.at[j], final_in, final_send.at[j], final_recv, r, first + j).wait_send()

    def near_copy(kb):
        return remote(
            b_ref.at[cols(first + kb), :], couple.at[cols(first + kb), cols(pos)],
            near_send.at[kb], near_recv.at[pos, kb], r, solver,
        )

    def far_copy(block):
        return remote(
            b_ref.at[pl.ds(block * wide, wide), :],
            couple.at[pl.ds(block * wide, wide), cols(pos)],
            far_send.at[block], far_recv.at[pos, block], r, solver,
        )

    def near_all():
        for kb in range(GROUP):
            @pl.when(kb <= pos)
            def _():
                near_copy(kb).start()

    def far_all():
        for block in range(last_group):
            @pl.when(block < g)
            def _():
                far_copy(block).start()

    def drain_all():
        for kb in range(GROUP):
            @pl.when(kb <= pos)
            def _():
                near_copy(kb).wait_send()
        for block in range(last_group):
            @pl.when(block < g)
            def _():
                far_copy(block).wait_send()

    def close():
        remote(final_in, final_in, final_send.at[0], final_recv, r, solver).wait_recv()
        norm_ref[...] = final_in[:, 0:bc]
        peak_ref[...] = final_in[:, bc:bc + br]

    def give(slot, j):
        return remote(partial_out.at[slot], partial.at[j], partial_send.at[slot], partial_recv.at[j], r, solver)

    def take_own(slot, h):
        remote(own.at[slot, piece(h)], own.at[slot, piece(h)], skip_send.at[0, h], own_recv.at[slot, h], r, solver).wait_recv()

    @pl.when(pos % 2 == 0)
    def _():
        greet(r, solver)

        @pl.when(pos == 0)
        def _():
            greet(r, first + GROUP - 1)

        @pl.when(pos > 0)
        def _():
            greet(r, c + 1)

        @pl.when(pos == PASS_FROM)
        def _():
            greet(r, first + PASS_TO)

        @pl.when(pos == PASS_TO)
        def _():
            greet(r, first + PASS_FROM)

        partial_out[1] = (2 * signs_ref[...] - 1).astype(BF16)

        @pl.when((pos == PASS_FROM) | (pos == PASS_TO))
        def _():
            pl.semaphore_wait(barrier, 3)

        @pl.when((pos != PASS_FROM) & (pos != PASS_TO))
        def _():
            pl.semaphore_wait(barrier, 2)

        def sign_zero():
            return remote(partial_out.at[1], sign_in.at[0], sign_send, sign_recv.at[0], r, first + GROUP - 1)

        def sign_next():
            return remote(partial_out.at[1], sign_in.at[1], sign_send, sign_recv.at[1], r, c + 1)

        def lend_near():
            return remote(b_ref.at[rows(g, wide), :], bounce_near, near_send.at[0], bounce_recv.at[n_group], r, first + PASS_TO)

        def lend_far(block):
            return remote(b_ref.at[pl.ds(block * wide, wide), :], bounce_far.at[block], far_send.at[block], bounce_recv.at[block], r, first + PASS_TO)

        def pass_near(kb):
            return remote(
                bounce_near.at[pl.ds(kb * bc, bc), :], couple.at[cols(first + kb), pl.ds(PASS_FROM * bc, bc)],
                bounce_send.at[kb], near_recv.at[PASS_FROM, kb], r, solver,
            )

        def pass_far(block):
            return remote(
                bounce_far.at[block], couple.at[pl.ds(block * wide, wide), pl.ds(PASS_FROM * bc, bc)],
                pass_send.at[block], far_recv.at[PASS_FROM, block], r, solver,
            )

        @pl.when((r < n_row - 2) & (pos == 0))
        def _():
            sign_zero().start()

        @pl.when((r < n_row - 2) & (pos > 0))
        def _():
            sign_next().start()

        @pl.when(pos != PASS_FROM)
        def _():
            far_all()

        for block in range(last_group):
            @pl.when((pos == PASS_FROM) & (block < g))
            def _():
                lend_far(block).start()

            @pl.when((pos == PASS_TO) & (block < g))
            def _():
                lend_far(block).wait_recv()
                pass_far(block).start()

        @pl.when(pos == PASS_FROM)
        def _():
            lend_near().start()

        @pl.when(pos != PASS_FROM)
        def _():
            near_all()

        @pl.when(r >= n_row - 2)
        def _():
            give(1, pos).start()

        @pl.when(pos == PASS_TO)
        def _():
            lend_near().wait_recv()
            for kb in range(PASS_FROM + 1):
                pass_near(kb).start()

        for h in range(PARTS):
            take_own(0, h)
        out_ref[...] = own[0]

        @pl.when(r < n_row - 2)
        def _():
            sign_next().wait_send()

        @pl.when(r >= n_row - 2)
        def _():
            give(1, pos).wait_send()

        @pl.when(pos == PASS_FROM)
        def _():
            lend_near().wait_send()
            for block in range(last_group):
                @pl.when(block < g)
                def _():
                    lend_far(block).wait_send()

        @pl.when(pos == PASS_TO)
        def _():
            for kb in range(PASS_FROM + 1):
                pass_near(kb).wait_send()
            for block in range(last_group):
                @pl.when(block < g)
                def _():
                    pass_far(block).wait_send()

        @pl.when(pos != PASS_FROM)
        def _():
            drain_all()

        close()

    @pl.when((pos % 2 == 1) & (pos > SOLVER))
    def _():
        upper = pos // half
        has_extra = pos % half == half - 1
        lag = upper

        def fetch():
            return pltpu.make_async_copy(a_ref, all_a, copy_a)

        greet(r, solver)
        greet(r, c - 1)
        for step in range(1, n_row):
            greet((r + step) % n_row, c)

        @pl.when(pos == GROUP - 1)
        def _():
            greet(r, first)

        fetch().start()
        signs = 2 * signs_ref[...] - 1
        total_own[2] = signs.astype(F32)
        partial_out[2] = signs.astype(BF16)

        @pl.when(pos == GROUP - 1)
        def _():
            pl.semaphore_wait(barrier, n_row + 2)

        @pl.when(pos < GROUP - 1)
        def _():
            pl.semaphore_wait(barrier, n_row + 1)

        far_all()
        near_all()

        @pl.when(r >= n_row - 2)
        def _():
            give(2, pos).start()


        @pl.when(r < n_row - 2)
        def _():
            remote(sign_in.at[1], sign_in.at[1], sign_send, sign_recv.at[1], r, c - 1).wait_recv()
            total_own[1] = sign_in[1].astype(F32)

            @pl.when(has_extra)
            def _():
                remote(sign_in.at[0], sign_in.at[0], sign_send, sign_recv.at[0], r, solver).wait_recv()
                total_own[0] = sign_in[0].astype(F32)

        fetch().wait()

        def lower_copy(slot, k, sems, row, h):
            return remote(lower.at[slot, k, piece(h)], lower.at[slot, k, piece(h)], sems.at[slot, k, h], lower_recv.at[slot, k, h], row, c)

        def relay_down(slot, k, h):
            return lower_copy(slot, k, down_send, (r + n_row - 1) % n_row, h)

        def relay_up(slot, k, h):
            return lower_copy(slot, k, up_send, (r + 1) % n_row, h)

        def skip(slot, h):
            return remote(own.at[slot, piece(h)], lower.at[slot, r, piece(h)], skip_send.at[slot, h], lower_recv.at[slot, r, h], (r + n_row - 2) % n_row, c)

        def wrap(slot, h):
            return remote(own.at[slot, piece(h)], lower.at[slot, r, piece(h)], wrap_send.at[slot, h], lower_recv.at[slot, r, h], 0, c)

        def forward(h):
            return remote(own.at[1, piece(h)], own.at[0, piece(h)], forward_send.at[h], own_recv.at[0, h], r, c - 1)

        def goes_down(k):
            return (k >= r + 2) & (k < r + DOWN) & (r > 0)

        def apply(slot, k):
            for h in range(PARTS):
                lower_copy(slot, k, down_send, (r + 1) % n_row, h).wait_recv()

                @pl.when(goes_down(k))
                def _():
                    relay_down(slot, k, h).start()

                @pl.when(k >= r + DOWN + 2)
                def _():
                    relay_up(slot, k, h).start()

            total_own[slot] -= dot(all_a[:, rows(k, br)], lower[slot, k])

        def handle(slot, k, j):
            @pl.when((k >= r + 2) & (k <= last_row))
            def _():
                apply(slot, k)

                @pl.when(k == r + 2)
                def _():
                    partial_out[slot] = total_own[slot].astype(BF16)
                    give(slot, j).start()

        def spread(slot):
            for h in range(PARTS):
                take_own(slot, h)

                @pl.when(r > 1)
                def _():
                    skip(slot, h).start()

                @pl.when(r > DOWN)
                def _():
                    wrap(slot, h).start()

        def event(i, carry):
            early = last_row - i
            late = last_row - i + lag

            @pl.when(has_extra)
            def _():
                handle(0, early, 1 - upper)

                @pl.when((early == r) & (r > 1))
                def _():
                    spread(0)

            handle(1, late, pos - 1)

            @pl.when(late == r)
            def _():
                spread(1)
                for h in range(PARTS):
                    forward(h).start()

            handle(2, late, pos)

            @pl.when(late == r)
            def _():
                spread(2)

            return carry

        lax.fori_loop(0, n_row + 2, event, 0)
        out_ref[...] = own[2]
        for h in range(PARTS):
            forward(h).wait_send()
        give(2, pos).wait_send()

        @pl.when(r < n_row - 2)
        def _():
            give(1, pos - 1).wait_send()

            @pl.when(has_extra)
            def _():
                give(0, 1 - upper).wait_send()

        def settle_slot(slot):
            def settle(i, carry):
                k = last_row - i

                @pl.when(goes_down(k))
                def _():
                    for h in range(PARTS):
                        relay_down(slot, k, h).wait_send()

                @pl.when(k >= r + DOWN + 2)
                def _():
                    for h in range(PARTS):
                        relay_up(slot, k, h).wait_send()

                return carry

            lax.fori_loop(0, n_row - 2, settle, 0)

            @pl.when(r > 1)
            def _():
                for h in range(PARTS):
                    skip(slot, h).wait_send()

            @pl.when(r > DOWN)
            def _():
                for h in range(PARTS):
                    wrap(slot, h).wait_send()

        @pl.when(has_extra)
        def _():
            settle_slot(0)

        settle_slot(1)
        settle_slot(2)
        drain_all()
        close()


def hand_out(solved_ref, norm_ref, peak_ref, solved_out, norm_out, peak_out):
    solved_out[...] = solved_ref[...]
    norm_out[...] = norm_ref[...]
    peak_out[...] = peak_ref[...]


def solution(mesh):
    n_row = mesh.shape["row"]
    n_col = mesh.shape["col"]

    def shards(signs, upper_a, upper_b, diag_inverse):
        br = diag_inverse.shape[0]
        bc = upper_b.shape[1]
        order = upper_b.shape[0]
        wide = GROUP * bc
        n_group = n_col // GROUP
        dma = pltpu.SemaphoreType.DMA
        vmem = pl.BlockSpec(memory_space=pltpu.VMEM)
        shapes = (
            jax.ShapeDtypeStruct((br, bc), BF16),
            jax.ShapeDtypeStruct((1, bc), F32),
            jax.ShapeDtypeStruct((1, br), F32),
        )
        results = pl.pallas_call(
            functools.partial(kernel, n_row, n_col),
            out_shape=shapes,
            in_specs=[vmem, pl.BlockSpec(memory_space=pl.ANY), vmem, vmem],
            out_specs=[vmem] * 3,
            scratch_shapes=[
                pltpu.VMEM((br, TERMS * br), BF16),
                pltpu.VMEM((order, wide), BF16),
                pltpu.VMEM((bc, (TERMS - 1) * bc), BF16),
                pltpu.VMEM((br, wide), BF16),
                pltpu.VMEM((GROUP, br, bc), BF16),
                pltpu.VMEM((GROUP, br, bc), BF16),
                pltpu.VMEM((GROUP, br, bc), BF16),
                pltpu.VMEM((n_col, br, bc), BF16),
                pltpu.VMEM((br, wide), F32),
                pltpu.VMEM((br, bc), F32),
                pltpu.VMEM((TERMS * br, bc), BF16),
                pltpu.VMEM((br, bc), F32),
                pltpu.VMEM((n_row, GROUP, bc), F32),
                pltpu.VMEM((n_group, 1, br), F32),
                pltpu.VMEM((GROUP, 1, bc + br), F32),
                pltpu.VMEM((br, br), BF16),
                pltpu.VMEM((3, br, bc), F32),
                pltpu.VMEM((3, n_row, br, bc), BF16),
                pltpu.VMEM((3, br, bc), BF16),
                pltpu.VMEM((3, br, bc), BF16),
                pltpu.VMEM((br, bc), BF16),
                pltpu.VMEM((2, br, bc), BF16),
                pltpu.VMEM((1, bc + br), F32),
                pltpu.VMEM((br, n_row * br), BF16),
                pltpu.VMEM((wide, bc), BF16),
                pltpu.VMEM((n_group, wide, bc), BF16),
                dma((GROUP,)), dma((GROUP, GROUP)),
                dma((n_group,)), dma((GROUP, n_group)),
                dma,
                dma, dma((2,)),
                dma((3,)), dma((GROUP,)),
                dma((GROUP, PARTS)), dma((GROUP, PARTS)),
                dma((GROUP,)), dma((n_col,)),
                dma((n_col,)),
                dma((GROUP, PARTS)), dma((3, PARTS)),
                dma((2, PARTS)),
                dma((3, n_row, PARTS)), dma((3, n_row, PARTS)), dma((3, n_row, PARTS)),
                dma((3, PARTS)), dma((3, PARTS)), dma((PARTS,)),
                dma((GROUP,)), dma((n_group + 1,)), dma((n_group,)),
                dma((n_row,)), dma((n_row,)),
                dma((n_group,)), dma((n_group,)),
                dma((GROUP,)), dma,
            ],
            compiler_params=pltpu.CompilerParams(
                collective_id=0, has_side_effects=True, vmem_limit_bytes=60 * 1024 * 1024
            ),
        )(signs[0], upper_a, upper_b, diag_inverse)
        solved, norms, peaks = pl.pallas_call(
            hand_out, out_shape=shapes, in_specs=[vmem] * 3, out_specs=[vmem] * 3
        )(*results)
        return solved[None], norms, peaks

    in_specs = (P(None, "row", "col"), P("row", None), P(None, "col"), P("row", None))
    out_specs = (P(None, "row", "col"), P(None, "col"), P(None, "row"))
    return jax.shard_map(shards, mesh=mesh, in_specs=in_specs, out_specs=out_specs, check_vma=False)
```

time: 172 us -> 156 us (0.907)
  Pallas kernels: 167 us -> 156 us
  local copies, waits for them, and re-layouts: 3.99 us -> 0 us
    pallas_call x1 -> x2, Pallas kernels: 167 us -> 156 us  [the longest x1 154 us: shards(): pl.pallas_call(functools.partial(kernel, n_row, n_col), out_shape=shapes,...]
    unnamed x3 -> x0, local copies, waits for them, and re-layouts: 3.99 us -> none
where the time goes in v2:
time: 156 us
  Pallas kernels  156 us (100%)
    pallas_call x1, Pallas kernels, shards(): pl.pallas_call(functools.partial(kernel, n_row, n_col), out_shape=shapes,...  154 us

profile of v2, /device:TPU:1, one launch (start us, length us, event | category | flops | bytes accessed | tf_op | source)
XLA Modules:
  0.0 156.3 jit_solution(9438616757755255496)
XLA Ops:
  0.6 154.1 %shard_map.67 = (bf16[512,128]{1,0:T(8,128)(2,1)}, f32[1,128]{1,0:T(1,128)}, f32[1,512]{1,0:T(1,128)}) custom-call(s32[512,128]{1,0:T(8,128)} %bitcast.2, bf16[512,4096]{1,0:T(8,128)(2,1)} %a_ref.1, bf16[4096,128]{1,0:T(8,128)(2,1)} %b_ref.1, bf16[512,512]{1,0:T(8,128)(2,1)} %d_ref.1), custom_call_target="tpu_custom_call" | custom-call | tf_op jit(solution)/shard_map/pallas_call | solution.py:705
  154.7 1.6 %shard_map.68 = (bf16[512,128]{1,0:T(8,128)(2,1)}, f32[1,128]{1,0:T(1,128)}, f32[1,512]{1,0:T(1,128)}) custom-call(bf16[512,128]{1,0:T(8,128)(2,1)} %get-tuple-element.9.solved_ref, f32[1,128]{1,0:T(1,128)} %get-tuple-element.10.norm_ref, f32[1,512]{1,0:T(1,128)} %get-tuple-element.11.peak_ref), custom_call_target="tpu_custom_call" | custom-call | tf_op jit(solution)/shard_map/pallas_call | solution.py:758

commit v3 on v2

--- a/solution.py
+++ b/solution.py
@@ -14,7 +14,7 @@
 PASS_FROM = 4
 PASS_TO = 2
 DOWN = 3
-PARTS = 2
+PARTS = 1
 TERMS = 4
 F32 = jnp.float32
 BF16 = jnp.bfloat16
@@ -102,7 +102,7 @@
         pl.semaphore_wait(barrier, GROUP - 1 + n_row - 1 + n_group - 1)
 
         def sign_copy():
-            return remote(sign_out, sign_in.at[0], sign_send, sign_recv.at[0], r, first + half - 1)
+            return remote(sign_out, sign_in.at[0], sign_send, sign_recv.at[0], r, first + half + 1)
 
         @pl.when(r < n_row - 2)
         def _():
@@ -181,8 +181,16 @@
             series[:, 0:bc] = -mine
             series[:, bc:2 * bc] = square
             series[:, 2 * bc:3 * bc] = (-dot(square, mine)).astype(BF16)
-            near = dot(strip[...], couple[rows(g, wide), cols(j)])
-            residual[...] = total[:, cols(j)] - near
+            mid = half * bc
+            from_left = pl.multiple_of(g * wide, wide)
+
+            @pl.when(j <= half)
+            def _():
+                residual[...] = total[:, cols(j)] - dot(strip[:, 0:mid], couple[pl.ds(from_left, mid), cols(j)])
+
+            @pl.when(j > half)
+            def _():
+                residual[...] = total[:, cols(j)] - dot(strip[...], couple[rows(g, wide), cols(j)])
 
             @pl.when((j != SOLVER) | (r < n_row - 2))
             def _():
@@ -214,11 +222,11 @@
                 def _():
                     @pl.when(j == SIDE)
                     def _():
-                        send_extra(SIDE, GROUP - 1, h).start()
+                        send_extra(SIDE, half - 1, h).start()
 
                     @pl.when(j == SOLVER)
                     def _():
-                        send_extra(SOLVER, half - 1, h).start()
+                        send_extra(SOLVER, half + 1, h).start()
 
                 @pl.when(j > SOLVER)
                 def _():
@@ -232,14 +240,18 @@
             def _():
                 send_right(j).start()
 
-            value = solved[j]
-            strip[:, cols(j)] = value
-            magnitude = jnp.abs(value.astype(F32))
+            strip[:, cols(j)] = solved[j]
+            return carry
+
+        lax.fori_loop(0, GROUP, column, 0)
+
+        def measure(j, carry):
+            magnitude = jnp.abs(solved[j].astype(F32))
             peaks[...] = jnp.maximum(peaks[...], magnitude)
             norm_all[r, pl.ds(j, 1), :] = jnp.sum(magnitude, axis=0, keepdims=True)
             return carry
 
-        lax.fori_loop(0, GROUP, column, 0)
+        lax.fori_loop(0, GROUP, measure, 0)
 
         peak_all[g] = jnp.max(jnp.transpose(peaks[...]), axis=0, keepdims=True)
         for step in range(1, n_row):
@@ -305,8 +317,8 @@
         @pl.when(r > 1)
         def _():
             for h in range(PARTS):
-                send_extra(SIDE, GROUP - 1, h).wait_send()
-                send_extra(SOLVER, half - 1, h).wait_send()
+                send_extra(SIDE, half - 1, h).wait_send()
+                send_extra(SOLVER, half + 1, h).wait_send()
 
         for step in range(1, n_row):
             remote(norm_all.at[r], norm_all.at[r], norm_send.at[step - 1], norm_recv.at[r], (r + step) % n_row, c).wait_send()
@@ -368,7 +380,7 @@
 
         @pl.when(pos == 0)
         def _():
-            greet(r, first + GROUP - 1)
+            greet(r, first + half - 1)
 
         @pl.when(pos > 0)
         def _():
@@ -393,7 +405,7 @@
             pl.semaphore_wait(barrier, 2)
 
         def sign_zero():
-            return remote(partial_out.at[1], sign_in.at[0], sign_send, sign_recv.at[0], r, first + GROUP - 1)
+            return remote(partial_out.at[1], sign_in.at[0], sign_send, sign_recv.at[0], r, first + half - 1)
 
         def sign_next():
             return remote(partial_out.at[1], sign_in.at[1], sign_send, sign_recv.at[1], r, c + 1)
@@ -493,9 +505,8 @@
 
     @pl.when((pos % 2 == 1) & (pos > SOLVER))
     def _():
-        upper = pos // half
-        has_extra = pos % half == half - 1
-        lag = upper
+        extra = pos // 2 - 1
+        has_extra = pos < GROUP - 1
 
         def fetch():
             return pltpu.make_async_copy(a_ref, all_a, copy_a)
@@ -505,7 +516,7 @@
         for step in range(1, n_row):
             greet((r + step) % n_row, c)
 
-        @pl.when(pos == GROUP - 1)
+        @pl.when(pos == half - 1)
         def _():
             greet(r, first)
 
@@ -514,11 +525,11 @@
         total_own[2] = signs.astype(F32)
         partial_out[2] = signs.astype(BF16)
 
-        @pl.when(pos == GROUP - 1)
+        @pl.when(pos == half - 1)
         def _():
             pl.semaphore_wait(barrier, n_row + 2)
 
-        @pl.when(pos < GROUP - 1)
+        @pl.when(pos != half - 1)
         def _():
             pl.semaphore_wait(barrier, n_row + 1)
 
@@ -601,11 +612,11 @@
 
         def event(i, carry):
             early = last_row - i
-            late = last_row - i + lag
+            late = last_row - i + 1
 
             @pl.when(has_extra)
             def _():
-                handle(0, early, 1 - upper)
+                handle(0, early, extra)
 
                 @pl.when((early == r) & (r > 1))
                 def _():
@@ -639,7 +650,7 @@
 
             @pl.when(has_extra)
             def _():
-                give(0, 1 - upper).wait_send()
+                give(0, extra).wait_send()
 
         def settle_slot(slot):
             def settle(i, carry):

time: 156 us -> 147 us (0.942)
  Pallas kernels: 156 us -> 146 us
    pallas_call x1, Pallas kernels: 154 us -> 144 us  [shards(): pl.pallas_call(functools.partial(kernel, n_row, n_col), out_shape=shapes,...]
where the time goes in v3:
time: 147 us; the launch traced here: 146 us
  Pallas kernels  146 us (99%)
    pallas_call x1, Pallas kernels, shards(): pl.pallas_call(functools.partial(kernel, n_row, n_col), out_shape=shapes,...  144 us

profile of v3, /device:TPU:1, one launch (start us, length us, event | category | flops | bytes accessed | tf_op | source)
XLA Modules:
  0.0 146.4 jit_solution(12882118060068571315)
XLA Ops:
  0.6 144.2 %shard_map.67 = (bf16[512,128]{1,0:T(8,128)(2,1)}, f32[1,128]{1,0:T(1,128)}, f32[1,512]{1,0:T(1,128)}) custom-call(s32[512,128]{1,0:T(8,128)} %bitcast.2, bf16[512,4096]{1,0:T(8,128)(2,1)} %a_ref.1, bf16[4096,128]{1,0:T(8,128)(2,1)} %b_ref.1, bf16[512,512]{1,0:T(8,128)(2,1)} %d_ref.1), custom_call_target="tpu_custom_call" | custom-call | tf_op jit(solution)/shard_map/pallas_call | solution.py:716
  144.8 1.6 %shard_map.68 = (bf16[512,128]{1,0:T(8,128)(2,1)}, f32[1,128]{1,0:T(1,128)}, f32[1,512]{1,0:T(1,128)}) custom-call(bf16[512,128]{1,0:T(8,128)(2,1)} %get-tuple-element.9.solved_ref, f32[1,128]{1,0:T(1,128)} %get-tuple-element.10.norm_ref, f32[1,512]{1,0:T(1,128)} %get-tuple-element.11.peak_ref), custom_call_target="tpu_custom_call" | custom-call | tf_op jit(solution)/shard_map/pallas_call | solution.py:769
